TPU v7x, 32 devices: a whole 2x2x4 slice. The times are simulated.
32 devices in a mesh: dp: 8 (over z, x), mp: 4 (over y, core).
Axes of the slice: x: 2, y: 2, z: 4, core: 2. Of those that a mesh axis runs over, the one named last changes fastest.
Arguments:
- vlm_tokens: bfloat16 [2048, 2048], P(('dp', 'mp')), may hold values from -64 to 64
- action_tokens: bfloat16 [4096, 2048], P(('dp', 'mp')), may hold values from -64 to 64
- norm_gain: float32 [2048], replicated, may hold values from 0.25 to 1.75
- proj_old: bfloat16 [4096, 4096], P('dp', 'mp'), may hold values from -0.125 to 0.125
Outputs:
- vlm_hidden: bfloat16 [4096, 4096], P('dp', 'mp')
- action_hidden: bfloat16 [4096, 8192], P('dp', 'mp')
- proj_new: bfloat16 [2048, 8192], P('dp', 'mp')
All inputs are finite; a program needn't handle non-finite values.
Results may differ from a plain program's by a relative error of at most 0.005.
Values may be sent and summed in bfloat16 or wider, within the bound.
A program may use at most 64 MiB of HBM per device.

v0:
```python
import functools
import math
import jax
import jax.numpy as jnp
from jax import lax
from jax.experimental import pallas as pl
from jax.experimental.pallas import tpu as pltpu
from jax.sharding import PartitionSpec as P

MESH = pl.DeviceIdType.MESH
epsilon = 1e-06


def column_plan(cols):
    wide = cols // 4
    narrow = max(wide // 2, 128)
    return ((0, wide, 3, 0), (3 * wide, narrow, wide // narrow, 3))


def number_of_chunks(cols):
    return sum(count for _, _, count, _ in column_plan(cols))


def normalize(row_values, norm_gain):
    values = row_values.astype(jnp.float32)
    factor = lax.rsqrt(jnp.mean(values * values, axis=-1, keepdims=True) + epsilon)
    return (values * factor * norm_gain).astype(jnp.bfloat16)


def gelu(u):
    return (u * 0.5 * (1.0 + lax.erf(u * math.sqrt(0.5)))).astype(jnp.bfloat16)


def kernel(groups, mp_size, vlm_hbm, act_hbm, gain_hbm, proj_hbm, vlm_out, act_out, new_out,
           vlm_ref, act_ref, gain_ref, tok, wbuf, hid, tok_send, tok_recv, w_send, w_recv, ex_send, ex_recv, hid_send, hid_recv, loc, load_sem,
           own_sem, vlm_sem, loc_w):
    d = lax.axis_index("dp")
    m = lax.axis_index("mp")
    g, p = d // 2, d % 2
    y, c = m // 2, m % 2
    vr, ar = vlm_ref.shape[0], act_ref.shape[0]
    r, cols = proj_hbm.shape
    half = r // 2
    plan = column_plan(cols)
    vlm_rows, act_rows = 2 * mp_size * vr, mp_size * ar
    sibling = (d, y * 2 + 1 - c)
    xpart = (g * 2 + 1 - p, m)
    ypart = (d, (1 - y) * 2 + c)
    has_left, has_right = g > 0, g < groups - 1

    def each_chunk(body, parts=plan):
        for first, width, count, base in parts:
            @pl.loop(0, count)
            def _(i):
                body(pl.ds(pl.multiple_of(first + i * width, width), width), base + i)

    barrier = pltpu.get_barrier_semaphore()

    @pl.when(has_left)
    def _():
        pl.semaphore_signal(barrier, inc=1, device_id=(d - 2, m), device_id_type=MESH)

    @pl.when(has_right)
    def _():
        pl.semaphore_signal(barrier, inc=1, device_id=(d + 2, m), device_id_type=MESH)

    for other in (xpart, ypart, sibling):
        pl.semaphore_signal(barrier, inc=1, device_id=other, device_id_type=MESH)

    def load_w(cc, k):
        return pltpu.make_async_copy(
            proj_hbm.at[:, cc], wbuf.at[pl.ds(pl.multiple_of(g * r, r), r), cc], loc_w.at[k])

    loads = [pltpu.make_async_copy(src, dst, load_sem.at[i]) for i, (src, dst) in enumerate(
        ((gain_hbm, gain_ref), (vlm_hbm, vlm_ref), (act_hbm, act_ref)))]
    each_chunk(lambda cc, k: load_w(cc, k).start())
    for load in loads:
        load.start()
    pl.semaphore_wait(barrier, 3 + has_left.astype(jnp.int32) + has_right.astype(jnp.int32))

    def w_copy(block, cc, k, side):
        rows = pl.ds(pl.multiple_of(block * r, r), r)
        return pltpu.make_async_remote_copy(
            src_ref=wbuf.at[rows, cc],
            dst_ref=wbuf.at[rows, cc],
            send_sem=w_send.at[side, block, k],
            recv_sem=w_recv.at[block, k],
            device_id=(d - 2 if side == 0 else d + 2, m),
            device_id_type=MESH,
        )

    def send_w(block, cc, k):
        @pl.when(has_left & (block >= g))
        def _():
            w_copy(block, cc, k, 0).start()

        @pl.when(has_right & (block <= g))
        def _():
            w_copy(block, cc, k, 1).start()

    def send_own(cc, k):
        load_w(cc, k).wait()
        send_w(g, cc, k)

    each_chunk(send_own)
    for load in loads:
        load.wait()

    def place(pp, mm):
        s = pp * mp_size + mm
        return (pl.ds(pl.multiple_of(s * vr, vr), vr), pl.ds(pl.multiple_of(vlm_rows + s * ar, ar), ar), s)

    step = 32

    @pl.loop(0, vr // step)
    def _(i):
        o = pl.multiple_of(i * step, step)
        tok[pl.ds(pl.multiple_of((p * mp_size + m) * vr + o, step), step), :] = normalize(
            vlm_ref[pl.ds(o, step), :], gain_ref[...])

    @pl.loop(0, ar // step)
    def _(i):
        o = pl.multiple_of(i * step, step)
        tok[pl.ds(pl.multiple_of(vlm_rows + (p * mp_size + m) * ar + o, step), step), :] = normalize(
            act_ref[pl.ds(o, step), :], gain_ref[...])

    def tok_copies(pp, mm, to, slot):
        va, aa, s = place(pp, mm)
        return [pltpu.make_async_remote_copy(
            src_ref=tok.at[rows, :], dst_ref=tok.at[rows, :], send_sem=tok_send.at[slot, j],
            recv_sem=tok_recv.at[s, j], device_id=to, device_id_type=MESH)
            for j, rows in enumerate((va, aa))]

    def tok_start(pp, mm, to, slot):
        for copy in tok_copies(pp, mm, to, slot):
            copy.start()

    def tok_arrive(pp, mm):
        for copy in tok_copies(pp, mm, sibling, 0):
            copy.wait_recv()

    m_y = (1 - y) * 2 + c
    m_s = y * 2 + 1 - c
    m_ys = (1 - y) * 2 + 1 - c
    tok_start(p, m, xpart, 0)
    tok_start(p, m, ypart, 1)
    tok_start(p, m, sibling, 2)

    ex = pltpu.make_async_remote_copy(
        src_ref=wbuf.at[pl.ds(pl.multiple_of(g * r + (1 - p) * half, half), half), :],
        dst_ref=new_out.at[:, pl.ds(pl.multiple_of(p * cols, cols), cols)],
        send_sem=ex_send, recv_sem=ex_recv, device_id=xpart, device_id_type=MESH)
    ex.start()
    kept = pltpu.make_async_copy(
        wbuf.at[pl.ds(pl.multiple_of(g * r + p * half, half), half), :],
        new_out.at[:, pl.ds(pl.multiple_of(p * cols, cols), cols)], loc)
    kept.start()

    def arrive(s, cc, k):
        @pl.when(g - s >= 0)
        def _():
            w_copy(g - s, cc, k, 1).wait_recv()
            send_w(g - s, cc, k)

        @pl.when(g + s < groups)
        def _():
            w_copy(g + s, cc, k, 0).wait_recv()
            send_w(g + s, cc, k)

    def phase(s, parts=plan):
        each_chunk(lambda cc, k: arrive(s, cc, k), parts)

    if groups > 2:
        phase(1, plan[:1])
    tok_arrive(1 - p, m)
    tok_start(1 - p, m, ypart, 3)
    tok_start(1 - p, m, sibling, 4)
    if groups > 2:
        phase(1, plan[1:])
    tok_arrive(p, m_y)
    tok_start(p, m_y, sibling, 5)
    tok_arrive(1 - p, m_y)
    tok_start(1 - p, m_y, sibling, 6)
    if groups > 3:
        @pl.loop(2, groups - 1)
        def _(s):
            phase(s)
    for pp, mm in ((p, m_s), (1 - p, m_s), (p, m_ys), (1 - p, m_ys)):
        tok_arrive(pp, mm)

    tile = math.gcd(256, math.gcd(vlm_rows, act_rows))
    a_tiles, v_tiles = act_rows // tile, vlm_rows // tile

    def out_cols(side, cc):
        return pl.ds(pl.multiple_of(side * cols + cc.start, cc.size), cc.size)

    def tile_rows(start):
        return pl.ds(pl.multiple_of(start, tile), tile)

    def hid_copy(cc, k, t):
        return pltpu.make_async_remote_copy(
            src_ref=hid.at[tile_rows(vlm_rows + (1 - p) * act_rows + t * tile), cc],
            dst_ref=act_out.at[tile_rows(t * tile), out_cols(p, cc)],
            send_sem=hid_send.at[k, t], recv_sem=hid_recv.at[k, t], device_id=xpart, device_id_type=MESH)

    def hid_back(cc, k, t):
        there = act_out.at[tile_rows(t * tile), out_cols(1 - p, cc)]
        return pltpu.make_async_remote_copy(
            src_ref=there, dst_ref=there, send_sem=hid_send.at[k, t], recv_sem=hid_recv.at[k, t],
            device_id=xpart, device_id_type=MESH)

    def own_copy(cc, k):
        return pltpu.make_async_copy(
            hid.at[pl.ds(pl.multiple_of(vlm_rows + p * act_rows, act_rows), act_rows), cc],
            act_out.at[:, out_cols(p, cc)], own_sem.at[k])

    def vlm_copy(cc, k):
        return pltpu.make_async_copy(hid.at[pl.ds(0, vlm_rows), cc], vlm_out.at[:, cc], vlm_sem.at[k])

    def hidden(rows, cc):
        pre = jnp.dot(tok[rows, :], wbuf[:, cc], preferred_element_type=jnp.float32)
        hid[rows, cc] = gelu(pre)

    def for_partner(cc, k):
        if groups > 1:
            arrive(groups - 1, cc, k)

        @pl.loop(0, a_tiles)
        def _(t):
            hidden(tile_rows(vlm_rows + (1 - p) * act_rows + t * tile), cc)
            hid_copy(cc, k, t).start()

    def for_self(cc, k):
        @pl.loop(0, a_tiles + v_tiles)
        def _(t):
            hidden(tile_rows(jnp.where(
                t < a_tiles, vlm_rows + p * act_rows + t * tile, (t - a_tiles) * tile)), cc)

            @pl.when(t == a_tiles - 1)
            def _():
                own_copy(cc, k).start()

        vlm_copy(cc, k).start()

    def for_both(cc, k):
        for_partner(cc, k)
        for_self(cc, k)

    first, width, count, base = plan[1]
    merged = ((first, width * count, 1, base),)
    each_chunk(for_both, plan[:1])
    each_chunk(for_partner, plan[1:])
    each_chunk(for_self, merged)

    to_of = ((p, m, xpart), (p, m, ypart), (p, m, sibling), (1 - p, m, ypart), (1 - p, m, sibling),
             (p, m_y, sibling), (1 - p, m_y, sibling))
    for slot, (pp, mm, to) in enumerate(to_of):
        for copy in tok_copies(pp, mm, to, slot):
            copy.wait_send()

    @pl.loop(0, groups)
    def _(block):
        def sent(cc, k):
            @pl.when(has_left & (block >= g))
            def _():
                w_copy(block, cc, k, 0).wait_send()

            @pl.when(has_right & (block <= g))
            def _():
                w_copy(block, cc, k, 1).wait_send()

        each_chunk(sent)

    ex.wait_send()
    taken = new_out.at[:, pl.ds(pl.multiple_of((1 - p) * cols, cols), cols)]
    pltpu.make_async_remote_copy(
        src_ref=taken, dst_ref=taken, send_sem=ex_send, recv_sem=ex_recv,
        device_id=xpart, device_id_type=MESH).wait_recv()
    kept.wait()

    def finish(cc, k):
        @pl.loop(0, a_tiles)
        def _(t):
            hid_copy(cc, k, t).wait_send()
            hid_back(cc, k, t).wait_recv()

    def stored(cc, k):
        own_copy(cc, k).wait()
        vlm_copy(cc, k).wait()

    each_chunk(stored, plan[:1] + merged)
    each_chunk(finish)


def store(*refs):
    count = (len(refs) - 1) // 2
    copies = [pltpu.make_async_copy(refs[i], refs[count + i], refs[-1].at[i]) for i in range(count)]
    for copy in copies:
        copy.start()
    for copy in copies:
        copy.wait()


def solution(mesh):
    groups, mp_size = mesh.shape["dp"] // 2, mesh.shape["mp"]

    def local(vlm_tokens, action_tokens, norm_gain, proj_old):
        vr, ar = vlm_tokens.shape[0], action_tokens.shape[0]
        features = vlm_tokens.shape[1]
        r, cols = proj_old.shape
        vlm_rows, act_rows = 2 * mp_size * vr, mp_size * ar
        bf16 = jnp.bfloat16
        dma = pltpu.SemaphoreType.DMA
        hbm, anywhere = pl.BlockSpec(memory_space=pltpu.HBM), pl.BlockSpec(memory_space=pl.ANY)
        chunks = number_of_chunks(cols)
        a_tiles = act_rows // math.gcd(256, math.gcd(vlm_rows, act_rows))
        shapes = (
            jax.ShapeDtypeStruct((vlm_rows, cols), bf16),
            jax.ShapeDtypeStruct((act_rows, 2 * cols), bf16),
            jax.ShapeDtypeStruct((r // 2, 2 * cols), bf16),
        )
        results = pl.pallas_call(
            functools.partial(kernel, groups, mp_size),
            name="up_gelu",
            out_shape=shapes,
            in_specs=[hbm] * 4,
            out_specs=(anywhere,) * 3,
            scratch_shapes=[
                pltpu.VMEM((vr, features), bf16),
                pltpu.VMEM((ar, features), bf16),
                pltpu.VMEM((1, features), jnp.float32),
                pltpu.VMEM((vlm_rows + 2 * act_rows, features), bf16),
                pltpu.VMEM((groups * r, cols), bf16),
                pltpu.VMEM((vlm_rows + 2 * act_rows, cols), bf16),
                dma((7, 2)), dma((2 * mp_size, 2)),
                dma((2, groups, chunks)), dma((groups, chunks)),
                dma, dma, dma((chunks, a_tiles)), dma((chunks, a_tiles)), dma, dma((3,)),
                dma((chunks,)), dma((chunks,)), dma((chunks,)),
            ],
            compiler_params=pltpu.CompilerParams(
                collective_id=0, has_side_effects=True, vmem_limit_bytes=48 * 1024 * 1024),
        )(*[pltpu.with_memory_space_constraint(array, pltpu.HBM) for array in (
            vlm_tokens, action_tokens, norm_gain.reshape(1, -1), proj_old)])
        return pl.pallas_call(
            store,
            name="store",
            out_shape=shapes,
            in_specs=[anywhere] * 3,
            out_specs=(hbm,) * 3,
            scratch_shapes=[dma((3,))],
            compiler_params=pltpu.CompilerParams(vmem_limit_bytes=1024 * 1024),
        )(*results)

    return jax.shard_map(
        local,
        mesh=mesh,
        in_specs=(P(("dp", "mp"), None), P(("dp", "mp"), None), P(), P("dp", "mp")),
        out_specs=(P("dp", "mp"), P("dp", "mp"), P("dp", "mp")),
        check_vma=False,
    )
```

profile of v0, /device:TPU:0, one launch (start us, length us, event | category | flops | bytes accessed | tf_op | source)
XLA Modules:
  0.0 83.8 jit_solution(17218352338595203863)
XLA Ops:
  0.6 81.1 %up_gelu.1 = (bf16[512,1024]{1,0:T(8,128)(2,1)S(1)}, bf16[512,2048]{1,0:T(8,128)(2,1)S(1)}, bf16[256,2048]{1,0:T(8,128)(2,1)S(1)}) custom-call(bf16[64,2048]{1,0:T(8,128)(2,1)} %vlm_hbm.1, bf16[128,2048]{1,0:T(8,128)(2,1)} %act_hbm.1, f32[1,2048]{1,0:T(1,128)} %bitcast.1, bf16[512,1024]{1,0:T(8,128)(2,1)} %proj_hbm.1), custom_call_target="tpu_custom_call" | custom-call | tf_op jit(solution)/shard_map/up_gelu/pallas_call | solution.py:322
  81.8 2.0 %store.1 = (bf16[512,1024]{1,0:T(8,128)(2,1)}, bf16[512,2048]{1,0:T(8,128)(2,1)}, bf16[256,2048]{1,0:T(8,128)(2,1)}) custom-call(bf16[512,1024]{1,0:T(8,128)(2,1)S(1)} %get-tuple-element.6.refs_0_, bf16[512,2048]{1,0:T(8,128)(2,1)S(1)} %get-tuple-element.7.refs_1_, bf16[256,2048]{1,0:T(8,128)(2,1)S(1)} %get-tuple-element.8.refs_2_), custom_call_target="tpu_custom_call" | custom-call | tf_op jit(solution)/shard_map/store/pallas_call | solution.py:344
where the time goes:
time: 83.9 us; the launch traced here: 83.8 us
  Pallas kernels  83.2 us (99%)
    pallas_call x1, Pallas kernels, local(): pl.pallas_call(functools.partial(kernel, groups, mp_size), name='up_gelu'...  81.1 us
    pallas_call x1, Pallas kernels, local(): pl.pallas_call(store, name='store', out_shape=shapes, in_specs=[anywhere]...  2.03 us

commit v1 on v0

v1 whole, which is shorter than its diff:
```python
import functools
import math
import jax
import jax.numpy as jnp
from jax import lax
from jax.experimental import pallas as pl
from jax.experimental.pallas import tpu as pltpu
from jax.sharding import PartitionSpec as P

MESH = pl.DeviceIdType.MESH
epsilon = 1e-06


def normalize(row_values, norm_gain):
    values = row_values.astype(jnp.float32)
    factor = lax.rsqrt(jnp.mean(values * values, axis=-1, keepdims=True) + epsilon)
    return (values * factor * norm_gain).astype(jnp.bfloat16)


def gelu(u):
    return (u * 0.5 * (1.0 + lax.erf(u * math.sqrt(0.5)))).astype(jnp.bfloat16)


def chunk_width(cols):
    return max(cols // 8, 128)


def kernel(groups, mp_size, vlm_hbm, act_hbm, gain_hbm, proj_hbm, vlm_out, act_out, new_out,
           vlm_ref, act_ref, gain_ref, tok, wbuf, hid, tok_send, tok_recv, w_send, w_recv, ex_send, ex_recv,
           hid_send, hid_recv, load_sem, loc_sem):
    d = lax.axis_index("dp")
    m = lax.axis_index("mp")
    g, p = d // 2, d % 2
    y, c = m // 2, m % 2
    vr, ar = vlm_ref.shape[0], act_ref.shape[0]
    r, cols = proj_hbm.shape
    half = r // 2
    width = chunk_width(cols)
    n = cols // width
    vlm_rows, act_rows = 2 * mp_size * vr, mp_size * ar
    sibling = (d, y * 2 + 1 - c)
    xpart = (g * 2 + 1 - p, m)
    ypart = (d, (1 - y) * 2 + c)
    has_left, has_right = g > 0, g < groups - 1

    def chunk(k, count=1):
        return pl.ds(pl.multiple_of(k * width, width), count * width)

    def block_rows(block):
        return pl.ds(pl.multiple_of(block * r, r), r)

    barrier = pltpu.get_barrier_semaphore()

    @pl.when(has_left)
    def _():
        pl.semaphore_signal(barrier, inc=1, device_id=(d - 2, m), device_id_type=MESH)

    @pl.when(has_right)
    def _():
        pl.semaphore_signal(barrier, inc=1, device_id=(d + 2, m), device_id_type=MESH)

    for other in (xpart, ypart, sibling):
        pl.semaphore_signal(barrier, inc=1, device_id=other, device_id_type=MESH)

    first_load = pltpu.make_async_copy(proj_hbm.at[:, chunk(0)], wbuf.at[block_rows(g), chunk(0)], load_sem.at[3])
    rest_load = pltpu.make_async_copy(
        proj_hbm.at[:, chunk(1, n - 1)], wbuf.at[block_rows(g), chunk(1, n - 1)], load_sem.at[4])
    loads = [pltpu.make_async_copy(src, dst, load_sem.at[i]) for i, (src, dst) in enumerate(
        ((gain_hbm, gain_ref), (vlm_hbm, vlm_ref), (act_hbm, act_ref)))]
    first_load.start()
    rest_load.start()
    for load in loads:
        load.start()
    pl.semaphore_wait(barrier, 3 + has_left.astype(jnp.int32) + has_right.astype(jnp.int32))

    def w_copy(block, cc, recv, side):
        return pltpu.make_async_remote_copy(
            src_ref=wbuf.at[block_rows(block), cc],
            dst_ref=wbuf.at[block_rows(block), cc],
            send_sem=w_send.at[side, block],
            recv_sem=recv,
            device_id=(d - 2 if side == 0 else d + 2, m),
            device_id_type=MESH,
        )

    def w_chunk(block, k, side):
        return w_copy(block, chunk(k), w_recv.at[block, k], side)

    def send_own(k):
        @pl.when(has_left)
        def _():
            w_chunk(g, k, 0).start()

        @pl.when(has_right)
        def _():
            w_chunk(g, k, 1).start()

    first_load.wait()
    send_own(0)
    rest_load.wait()
    send_own(1)
    for load in loads:
        load.wait()

    def token_rows(pp, mm):
        s = pp * mp_size + mm
        return (pl.ds(pl.multiple_of(s * vr, vr), vr), pl.ds(pl.multiple_of(vlm_rows + s * ar, ar), ar))

    step = 32

    @pl.loop(0, vr // step)
    def _(i):
        o = pl.multiple_of(i * step, step)
        tok[pl.ds(pl.multiple_of((p * mp_size + m) * vr + o, step), step), :] = normalize(
            vlm_ref[pl.ds(o, step), :], gain_ref[...])

    @pl.loop(0, ar // step)
    def _(i):
        o = pl.multiple_of(i * step, step)
        tok[pl.ds(pl.multiple_of(vlm_rows + (p * mp_size + m) * ar + o, step), step), :] = normalize(
            act_ref[pl.ds(o, step), :], gain_ref[...])

    def tok_copy(pp, mm, part, to, slot):
        rows = token_rows(pp, mm)[part]
        return pltpu.make_async_remote_copy(
            src_ref=tok.at[rows, :], dst_ref=tok.at[rows, :], send_sem=tok_send,
            recv_sem=tok_recv.at[slot, 0 if slot == 3 else part], device_id=to, device_id_type=MESH)

    m_y = (1 - y) * 2 + c
    for part in (1, 0):
        tok_copy(p, m, part, xpart, 0).start()
        tok_copy(p, m, part, ypart, 1).start()
    for part in (1, 0):
        tok_copy(p, m, part, sibling, 3).start()

    def relay_first():
        tok_copy(1 - p, m, 1, sibling, 0).wait_recv()
        tok_copy(1 - p, m, 1, ypart, 2).start()
        tok_copy(p, m_y, 1, sibling, 1).wait_recv()
        tok_copy(p, m_y, 0, sibling, 1).wait_recv()
        tok_copy(p, m_y, 0, xpart, 2).start()
        tok_copy(1 - p, m, 0, sibling, 0).wait_recv()
        for part in (1, 0):
            tok_copy(1 - p, m, part, sibling, 3).start()
            tok_copy(p, m_y, part, sibling, 3).start()

    def relay_second():
        for part in (0, 1):
            tok_copy(1 - p, m_y, part, sibling, 2).wait_recv()
            tok_copy(1 - p, m_y, part, sibling, 3).start()

    def all_tokens():
        count = mp_size * (vr + ar)
        there = tok.at[pl.ds(0, count), :]
        pltpu.make_async_remote_copy(
            src_ref=there, dst_ref=there, send_sem=tok_send, recv_sem=tok_recv.at[3, 0],
            device_id=sibling, device_id_type=MESH).wait_recv()

    ex = pltpu.make_async_remote_copy(
        src_ref=wbuf.at[pl.ds(pl.multiple_of(g * r + (1 - p) * half, half), half), :],
        dst_ref=new_out.at[:, pl.ds(pl.multiple_of(p * cols, cols), cols)],
        send_sem=ex_send, recv_sem=ex_recv, device_id=xpart, device_id_type=MESH)
    kept = pltpu.make_async_copy(
        wbuf.at[pl.ds(pl.multiple_of(g * r + p * half, half), half), :],
        new_out.at[:, pl.ds(pl.multiple_of(p * cols, cols), cols)], loc_sem.at[0])

    def arrive(t):
        own = t + 2 if isinstance(t, int) else t + 2

        @pl.when(own < n)
        def _():
            send_own(own)

        @pl.loop(0, groups - 1)
        def _(i):
            k = t - i

            @pl.when((k >= 0) & (k < n) & (g - 1 - i >= 0))
            def _():
                w_chunk(g - 1 - i, k, 1).wait_recv()

                @pl.when(has_right)
                def _():
                    w_chunk(g - 1 - i, k, 1).start()

            @pl.when((k >= 0) & (k < n) & (g + 1 + i < groups))
            def _():
                w_chunk(g + 1 + i, k, 0).wait_recv()

                @pl.when(has_left)
                def _():
                    w_chunk(g + 1 + i, k, 0).start()

    tile = math.gcd(256, math.gcd(vlm_rows, act_rows))
    a_tiles, v_tiles = act_rows // tile, vlm_rows // tile

    def out_cols(side, cc):
        return pl.ds(pl.multiple_of(side * cols + cc.start, cc.size), cc.size)

    def tile_rows(start):
        return pl.ds(pl.multiple_of(start, tile), tile)

    def hid_copy(cc, t):
        return pltpu.make_async_remote_copy(
            src_ref=hid.at[tile_rows(vlm_rows + (1 - p) * act_rows + t * tile), cc],
            dst_ref=act_out.at[tile_rows(t * tile), out_cols(p, cc)],
            send_sem=hid_send, recv_sem=hid_recv, device_id=xpart, device_id_type=MESH)

    def own_copy(cc):
        return pltpu.make_async_copy(
            hid.at[pl.ds(pl.multiple_of(vlm_rows + p * act_rows, act_rows), act_rows), cc],
            act_out.at[:, out_cols(p, cc)], loc_sem.at[1])

    def vlm_copy(cc):
        return pltpu.make_async_copy(hid.at[pl.ds(0, vlm_rows), cc], vlm_out.at[:, cc], loc_sem.at[2])

    def hidden(rows, cc):
        pre = jnp.dot(tok[rows, :], wbuf[:, cc], preferred_element_type=jnp.float32)
        hid[rows, cc] = gelu(pre)

    def for_partner(cc):
        @pl.loop(0, a_tiles)
        def _(t):
            hidden(tile_rows(vlm_rows + (1 - p) * act_rows + t * tile), cc)
            hid_copy(cc, t).start()

    def for_self(cc):
        @pl.loop(0, a_tiles + v_tiles)
        def _(t):
            hidden(tile_rows(jnp.where(
                t < a_tiles, vlm_rows + p * act_rows + t * tile, (t - a_tiles) * tile)), cc)

    warm = groups - 1

    @pl.loop(0, warm)
    def _(t):
        arrive(t)

    relay_first()
    ex.start()
    kept.start()
    arrive(warm)
    arrive(warm + 1)
    relay_second()
    all_tokens()
    for j in range(0, n - 2, 2):
        if j:
            for t in (warm + j - 1, warm + j):
                if t > warm + 1:
                    arrive(t)
        for_partner(chunk(j, 2))
        for_self(chunk(j, 2))
    for j in (n - 2, n - 1):
        arrive(warm + j - 1)
        for_partner(chunk(j))
    for_self(chunk(n - 2, 2))
    own_copy(pl.ds(0, cols)).start()
    vlm_copy(pl.ds(0, cols)).start()

    count = 7 * (vr + ar)
    sent = tok.at[pl.ds(0, count), :]
    pltpu.make_async_remote_copy(
        src_ref=sent, dst_ref=sent, send_sem=tok_send, recv_sem=tok_recv.at[3, 0],
        device_id=sibling, device_id_type=MESH).wait_send()

    @pl.loop(0, groups)
    def _(block):
        @pl.when(has_left & (block >= g))
        def _():
            w_copy(block, pl.ds(0, cols), w_recv.at[block, 0], 0).wait_send()

        @pl.when(has_right & (block <= g))
        def _():
            w_copy(block, pl.ds(0, cols), w_recv.at[block, 0], 1).wait_send()

    ex.wait_send()
    taken = new_out.at[:, pl.ds(pl.multiple_of((1 - p) * cols, cols), cols)]
    pltpu.make_async_remote_copy(
        src_ref=taken, dst_ref=taken, send_sem=ex_send, recv_sem=ex_recv,
        device_id=xpart, device_id_type=MESH).wait_recv()
    kept.wait()
    own_copy(pl.ds(0, cols)).wait()
    vlm_copy(pl.ds(0, cols)).wait()
    there = act_out.at[:, pl.ds(pl.multiple_of((1 - p) * cols, cols), cols)]
    back = pltpu.make_async_remote_copy(
        src_ref=there, dst_ref=there, send_sem=hid_send, recv_sem=hid_recv,
        device_id=xpart, device_id_type=MESH)
    back.wait_send()
    back.wait_recv()


def store(*refs):
    count = (len(refs) - 1) // 2
    copies = [pltpu.make_async_copy(refs[i], refs[count + i], refs[-1].at[i]) for i in range(count)]
    for copy in copies:
        copy.start()
    for copy in copies:
        copy.wait()


def solution(mesh):
    groups, mp_size = mesh.shape["dp"] // 2, mesh.shape["mp"]

    def local(vlm_tokens, action_tokens, norm_gain, proj_old):
        vr, ar = vlm_tokens.shape[0], action_tokens.shape[0]
        features = vlm_tokens.shape[1]
        r, cols = proj_old.shape
        vlm_rows, act_rows = 2 * mp_size * vr, mp_size * ar
        bf16 = jnp.bfloat16
        dma = pltpu.SemaphoreType.DMA
        hbm, anywhere = pl.BlockSpec(memory_space=pltpu.HBM), pl.BlockSpec(memory_space=pl.ANY)
        chunks = cols // chunk_width(cols)
        shapes = (
            jax.ShapeDtypeStruct((vlm_rows, cols), bf16),
            jax.ShapeDtypeStruct((act_rows, 2 * cols), bf16),
            jax.ShapeDtypeStruct((r // 2, 2 * cols), bf16),
        )
        results = pl.pallas_call(
            functools.partial(kernel, groups, mp_size),
            name="up_gelu",
            out_shape=shapes,
            in_specs=[hbm] * 4,
            out_specs=(anywhere,) * 3,
            scratch_shapes=[
                pltpu.VMEM((vr, features), bf16),
                pltpu.VMEM((ar, features), bf16),
                pltpu.VMEM((1, features), jnp.float32),
                pltpu.VMEM((vlm_rows + 2 * act_rows, features), bf16),
                pltpu.VMEM((groups * r, cols), bf16),
                pltpu.VMEM((vlm_rows + 2 * act_rows, cols), bf16),
                dma, dma((4, 2)), dma((2, groups)), dma((groups, chunks)), dma, dma, dma, dma, dma((5,)), dma((3,)),
            ],
            compiler_params=pltpu.CompilerParams(
                collective_id=0, has_side_effects=True, vmem_limit_bytes=48 * 1024 * 1024),
        )(*[pltpu.with_memory_space_constraint(array, pltpu.HBM) for array in (
            vlm_tokens, action_tokens, norm_gain.reshape(1, -1), proj_old)])
        return pl.pallas_call(
            store,
            name="store",
            out_shape=shapes,
            in_specs=[anywhere] * 3,
            out_specs=(hbm,) * 3,
            scratch_shapes=[dma((3,))],
            compiler_params=pltpu.CompilerParams(vmem_limit_bytes=1024 * 1024),
        )(*results)

    return jax.shard_map(
        local,
        mesh=mesh,
        in_specs=(P(("dp", "mp"), None), P(("dp", "mp"), None), P(), P("dp", "mp")),
        out_specs=(P("dp", "mp"), P("dp", "mp"), P("dp", "mp")),
        check_vma=False,
    )
```

time: 83.9 us -> 81.9 us (0.976)
  Pallas kernels: 83.2 us -> 81.1 us
    pallas_call x1, Pallas kernels: 81.1 us -> 79 us  [local(): pl.pallas_call(functools.partial(kernel, groups, mp_size), name='up_gelu'...]
where the time goes in v1:
time: 81.9 us; the launch traced here: 81.7 us
  Pallas kernels  81.1 us (99%)
    pallas_call x1, Pallas kernels, local(): pl.pallas_call(functools.partial(kernel, groups, mp_size), name='up_gelu'...  79 us
    pallas_call x1, Pallas kernels, local(): pl.pallas_call(store, name='store', out_shape=shapes, in_specs=[anywhere]...  2.03 us

profile of v1, /device:TPU:0, one launch (start us, length us, event | category | flops | bytes accessed | tf_op | source)
XLA Modules:
  0.0 81.7 jit_solution(3205826926757695933)
XLA Ops:
  0.6 79.0 %up_gelu.1 = (bf16[512,1024]{1,0:T(8,128)(2,1)S(1)}, bf16[512,2048]{1,0:T(8,128)(2,1)S(1)}, bf16[256,2048]{1,0:T(8,128)(2,1)S(1)}) custom-call(bf16[64,2048]{1,0:T(8,128)(2,1)} %vlm_hbm.1, bf16[128,2048]{1,0:T(8,128)(2,1)} %act_hbm.1, f32[1,2048]{1,0:T(1,128)} %bitcast.1, bf16[512,1024]{1,0:T(8,128)(2,1)} %proj_hbm.1), custom_call_target="tpu_custom_call" | custom-call | tf_op jit(solution)/shard_map/up_gelu/pallas_call | solution.py:318
  79.7 2.0 %store.1 = (bf16[512,1024]{1,0:T(8,128)(2,1)}, bf16[512,2048]{1,0:T(8,128)(2,1)}, bf16[256,2048]{1,0:T(8,128)(2,1)}) custom-call(bf16[512,1024]{1,0:T(8,128)(2,1)S(1)} %get-tuple-element.6.refs_0_, bf16[512,2048]{1,0:T(8,128)(2,1)S(1)} %get-tuple-element.7.refs_1_, bf16[256,2048]{1,0:T(8,128)(2,1)S(1)} %get-tuple-element.8.refs_2_), custom_call_target="tpu_custom_call" | custom-call | tf_op jit(solution)/shard_map/store/pallas_call | solution.py:337

commit v2 on v1

--- a/solution.py
+++ b/solution.py
@@ -27,7 +27,8 @@
 
 def kernel(groups, mp_size, vlm_hbm, act_hbm, gain_hbm, proj_hbm, vlm_out, act_out, new_out,
            vlm_ref, act_ref, gain_ref, tok, wbuf, hid, tok_send, tok_recv, w_send, w_recv, ex_send, ex_recv,
-           hid_send, hid_recv, load_sem, loc_sem):
+           hid_send, hid_recv, load_sem, loc_sem, far_tok, far_w, far_hid, ft_send, ft_recv, fw_send, fw_recv,
+           fh_send, fh_recv):
     d = lax.axis_index("dp")
     m = lax.axis_index("mp")
     g, p = d // 2, d % 2
@@ -42,6 +43,12 @@
     xpart = (g * 2 + 1 - p, m)
     ypart = (d, (1 - y) * 2 + c)
     has_left, has_right = g > 0, g < groups - 1
+    far = groups >= 4 and n >= 8
+    end = (g == 0) | (g == groups - 1)
+    near = ((g == 1) | (g == groups - 2)) & far
+    short = end & (c == 0) & far
+    toward = jnp.where(g <= 1, 0, groups - 1)
+    inward = jnp.where(g == 0, 1, groups - 2)
 
     def chunk(k, count=1):
         return pl.ds(pl.multiple_of(k * width, width), count * width)
@@ -71,34 +78,58 @@
     rest_load.start()
     for load in loads:
         load.start()
-    pl.semaphore_wait(barrier, 3 + has_left.astype(jnp.int32) + has_right.astype(jnp.int32))
+
+    @pl.when(near & (c == 1))
+    def _():
+        pl.semaphore_signal(barrier, inc=1, device_id=(toward * 2 + p, y * 2), device_id_type=MESH)
+
+    pl.semaphore_wait(barrier, 3 + sum(flag.astype(jnp.int32) for flag in (has_left, has_right, short)))
 
     def w_copy(block, cc, recv, side):
         return pltpu.make_async_remote_copy(
             src_ref=wbuf.at[block_rows(block), cc],
             dst_ref=wbuf.at[block_rows(block), cc],
-            send_sem=w_send.at[side, block],
+            send_sem=w_send.at[jnp.where((block == g) & (side == 0), groups, block)],
             recv_sem=recv,
             device_id=(d - 2 if side == 0 else d + 2, m),
             device_id_type=MESH,
         )
 
     def w_chunk(block, k, side):
-        return w_copy(block, chunk(k), w_recv.at[block, k], side)
+        return w_copy(block, chunk(k), w_recv.at[lax.rem(block - g + 2 * groups + (0 if side == 0 else -2), groups), k], side)
+
+    def w_arrival(block, k):
+        there = wbuf.at[block_rows(block), chunk(k)]
+        return pltpu.make_async_remote_copy(
+            src_ref=there, dst_ref=there, send_sem=w_send.at[block],
+            recv_sem=w_recv.at[lax.rem(block - g + 2 * groups - 1, groups), k],
+            device_id=sibling, device_id_type=MESH)
+
+    short_left = near & (g == 1) & (c == 0)
+    short_right = near & (g == groups - 2) & (c == 0)
+
+    def send_w(block, k, side):
+        ok, brief = (has_left, short_left) if side == 0 else (has_right, short_right)
+
+        @pl.when(ok & jnp.logical_not(brief & (k == 0)))
+        def _():
+            w_chunk(block, k, side).start()
 
     def send_own(k):
-        @pl.when(has_left)
-        def _():
-            w_chunk(g, k, 0).start()
-
-        @pl.when(has_right)
-        def _():
-            w_chunk(g, k, 1).start()
+        send_w(g, k, 0)
+        send_w(g, k, 1)
 
     first_load.wait()
     send_own(0)
     rest_load.wait()
     send_own(1)
+
+    @pl.when(end)
+    def _():
+        @pl.loop(2, n)
+        def _(k):
+            send_own(k)
+
     for load in loads:
         load.wait()
 
@@ -132,6 +163,81 @@
         tok_copy(p, m, part, ypart, 1).start()
     for part in (1, 0):
         tok_copy(p, m, part, sibling, 3).start()
+
+    def far_token_copy(part, c_from):
+        rows = token_rows(p, m)[part]
+        at = pl.ds(pl.multiple_of(c_from * (vr + ar) + part * vr, math.gcd(vr, ar)), (vr, ar)[part])
+        return pltpu.make_async_remote_copy(
+            src_ref=tok.at[rows, :], dst_ref=far_tok.at[at, :], send_sem=ft_send, recv_sem=ft_recv,
+            device_id=(inward * 2 + p, y * 2 + 1), device_id_type=MESH)
+
+    if far:
+        @pl.when(end)
+        def _():
+            for part in (0, 1):
+                far_token_copy(part, c).start()
+
+    def far_w_copy(panel, to, slot):
+        at = far_w.at[:, pl.ds(pl.multiple_of(panel * width, width), width)]
+        return pltpu.make_async_remote_copy(
+            src_ref=at if slot == 3 else wbuf.at[:, chunk(0)], dst_ref=at, send_sem=fw_send, recv_sem=fw_recv.at[slot],
+            device_id=to, device_id_type=MESH)
+
+    def spread_far_w():
+        @pl.when(near & (c == 0))
+        def _():
+            far_w_copy(y * 2 + p, (g * 2 + 1 - p, y * 2 + 1), 1).start()
+            far_w_copy(y * 2 + p, (d, (1 - y) * 2 + 1), 2).start()
+            far_w_copy(y * 2 + p, sibling, 0).start()
+
+    def relay_far_w():
+        @pl.when(near & (c == 1))
+        def _():
+            far_w_copy(y * 2 + 1 - p, ypart, 1).wait_recv()
+            far_w_copy(y * 2 + 1 - p, ypart, 3).start()
+
+    def far_hid_copies(same_chip):
+        for c_from in (0, 1):
+            base = c_from * (vr + ar)
+            m_from = y * 2 + c_from
+            for step_y in (0, 1):
+                y_to = y if step_y == 0 else 1 - y
+                for step_p in (0, 1):
+                    b = p if step_p == 0 else 1 - p
+                    cols_at = pl.ds(pl.multiple_of((y_to * 2 + b) * width, width), width)
+                    if (step_y == 0 and step_p == 0) == same_chip:
+                        yield pltpu.make_async_remote_copy(
+                            src_ref=far_hid.at[pl.ds(base, vr), cols_at],
+                            dst_ref=vlm_out.at[pl.ds(pl.multiple_of((p * mp_size + m_from) * vr, vr), vr), chunk(0)],
+                            send_sem=fh_send, recv_sem=fh_recv, device_id=(toward * 2 + b, y_to * 2), device_id_type=MESH)
+                    if (step_y == 0) == same_chip:
+                        yield pltpu.make_async_remote_copy(
+                            src_ref=far_hid.at[pl.ds(base + vr, ar), cols_at],
+                            dst_ref=act_out.at[pl.ds(pl.multiple_of(m_from * ar, ar), ar), out_cols(b, chunk(0))],
+                            send_sem=fh_send, recv_sem=fh_recv, device_id=(toward * 2 + p, y_to * 2), device_id_type=MESH)
+
+    def far_compute():
+        @pl.when(near & (c == 1))
+        def _():
+            pltpu.make_async_remote_copy(
+                src_ref=far_tok, dst_ref=far_tok, send_sem=ft_send, recv_sem=ft_recv,
+                device_id=sibling, device_id_type=MESH).wait_recv()
+            far_w_copy(y * 2, sibling, 0).wait_recv()
+            far_w_copy(y * 2, sibling, 2).wait_recv()
+            far_w_copy(y * 2, sibling, 3).wait_recv()
+
+            @pl.loop(0, 2)
+            def _(i):
+                rows = pl.ds(pl.multiple_of(i * (vr + ar), math.gcd(vr, ar)), vr + ar)
+
+                @pl.loop(0, 2)
+                def _(j):
+                    at = pl.ds(pl.multiple_of(j * 2 * width, width), 2 * width)
+                    pre = jnp.dot(far_tok[rows, :], far_w[:, at], preferred_element_type=jnp.float32)
+                    far_hid[rows, at] = gelu(pre)
+
+            for copy in far_hid_copies(True):
+                copy.start()
 
     def relay_first():
         tok_copy(1 - p, m, 1, sibling, 0).wait_recv()
@@ -165,37 +271,31 @@
         new_out.at[:, pl.ds(pl.multiple_of(p * cols, cols), cols)], loc_sem.at[0])
 
     def arrive(t):
-        own = t + 2 if isinstance(t, int) else t + 2
-
-        @pl.when(own < n)
-        def _():
-            send_own(own)
+        @pl.when((t + 2 < n) & jnp.logical_not(end))
+        def _():
+            send_own(t + 2)
 
         @pl.loop(0, groups - 1)
         def _(i):
             k = t - i
 
-            @pl.when((k >= 0) & (k < n) & (g - 1 - i >= 0))
+            inside = (k >= 0) & (k < n) & jnp.logical_not(short & (k == 0))
+
+            @pl.when(inside & (g - 1 - i >= 0))
             def _():
-                w_chunk(g - 1 - i, k, 1).wait_recv()
-
-                @pl.when(has_right)
-                def _():
-                    w_chunk(g - 1 - i, k, 1).start()
-
-            @pl.when((k >= 0) & (k < n) & (g + 1 + i < groups))
+                w_arrival(g - 1 - i, k).wait_recv()
+                send_w(g - 1 - i, k, 1)
+
+            @pl.when(inside & (g + 1 + i < groups))
             def _():
-                w_chunk(g + 1 + i, k, 0).wait_recv()
-
-                @pl.when(has_left)
-                def _():
-                    w_chunk(g + 1 + i, k, 0).start()
+                w_arrival(g + 1 + i, k).wait_recv()
+                send_w(g + 1 + i, k, 0)
 
     tile = math.gcd(256, math.gcd(vlm_rows, act_rows))
     a_tiles, v_tiles = act_rows // tile, vlm_rows // tile
 
     def out_cols(side, cc):
-        return pl.ds(pl.multiple_of(side * cols + cc.start, cc.size), cc.size)
+        return pl.ds(pl.multiple_of(side * cols + cc.start, width), cc.size)
 
     def tile_rows(start):
         return pl.ds(pl.multiple_of(start, tile), tile)
@@ -237,56 +337,115 @@
         arrive(t)
 
     relay_first()
+    if far:
+        spread_far_w()
     ex.start()
     kept.start()
     arrive(warm)
     arrive(warm + 1)
     relay_second()
+    if far:
+        relay_far_w()
     all_tokens()
-    for j in range(0, n - 2, 2):
-        if j:
-            for t in (warm + j - 1, warm + j):
-                if t > warm + 1:
-                    arrive(t)
+
+    def first_pair():
+        if far:
+            @pl.when(short)
+            def _():
+                for_partner(chunk(1))
+                for_self(chunk(1))
+
+            @pl.when(jnp.logical_not(short))
+            def _():
+                for_partner(chunk(0, 2))
+                for_self(chunk(0, 2))
+        else:
+            for_partner(chunk(0, 2))
+            for_self(chunk(0, 2))
+
+    first_pair()
+    for j in range(2, n - 2, 2):
+        for t in (warm + j - 1, warm + j):
+            if t > warm + 1:
+                arrive(t)
         for_partner(chunk(j, 2))
         for_self(chunk(j, 2))
-    for j in (n - 2, n - 1):
-        arrive(warm + j - 1)
-        for_partner(chunk(j))
+    arrive(warm + n - 3)
+    for_partner(chunk(n - 2))
+    arrive(warm + n - 2)
+    if far:
+        far_compute()
+    for_partner(chunk(n - 1))
     for_self(chunk(n - 2, 2))
-    own_copy(pl.ds(0, cols)).start()
-    vlm_copy(pl.ds(0, cols)).start()
-
-    count = 7 * (vr + ar)
-    sent = tok.at[pl.ds(0, count), :]
-    pltpu.make_async_remote_copy(
-        src_ref=sent, dst_ref=sent, send_sem=tok_send, recv_sem=tok_recv.at[3, 0],
-        device_id=sibling, device_id_type=MESH).wait_send()
+
+    tail_cols, all_cols = chunk(1, n - 1), chunk(0, n)
+
+    def by_width(brief, body):
+        @pl.when(brief)
+        def _():
+            body(tail_cols)
+
+        @pl.when(jnp.logical_not(brief))
+        def _():
+            body(all_cols)
+
+    def copy_out(cc):
+        own_copy(cc).start()
+        vlm_copy(cc).start()
+
+    def copied_out(cc):
+        own_copy(cc).wait()
+        vlm_copy(cc).wait()
+
+    by_width(short, copy_out)
 
     @pl.loop(0, groups)
     def _(block):
         @pl.when(has_left & (block >= g))
         def _():
-            w_copy(block, pl.ds(0, cols), w_recv.at[block, 0], 0).wait_send()
+            by_width(short_left, lambda cc: w_copy(block, cc, ex_recv, 0).wait_send())
 
         @pl.when(has_right & (block <= g))
         def _():
-            w_copy(block, pl.ds(0, cols), w_recv.at[block, 0], 1).wait_send()
-
+            by_width(short_right, lambda cc: w_copy(block, cc, ex_recv, 1).wait_send())
+
+    def bytes_of(ref, send, recv):
+        return pltpu.make_async_remote_copy(
+            src_ref=ref, dst_ref=ref, send_sem=send, recv_sem=recv, device_id=sibling, device_id_type=MESH)
+
+    if far:
+        @pl.when(near & (c == 1))
+        def _():
+            for copy in far_hid_copies(False):
+                copy.start()
+            bytes_of(far_w.at[:, pl.ds(0, width)], fw_send, ex_recv).wait_send()
+            bytes_of(hid.at[pl.ds(0, 8 * (vr + ar)), chunk(0)], fh_send, ex_recv).wait_send()
+
+        @pl.when(near & (c == 0))
+        def _():
+            bytes_of(wbuf.at[:, pl.ds(0, 3 * width)], fw_send, ex_recv).wait_send()
+
+        @pl.when(end)
+        def _():
+            bytes_of(tok.at[pl.ds(0, vr + ar), :], ft_send, ex_recv).wait_send()
+
+    bytes_of(tok.at[pl.ds(0, 7 * (vr + ar)), :], tok_send, ex_recv).wait_send()
     ex.wait_send()
     taken = new_out.at[:, pl.ds(pl.multiple_of((1 - p) * cols, cols), cols)]
-    pltpu.make_async_remote_copy(
-        src_ref=taken, dst_ref=taken, send_sem=ex_send, recv_sem=ex_recv,
-        device_id=xpart, device_id_type=MESH).wait_recv()
+    bytes_of(taken, ex_send, ex_recv).wait_recv()
     kept.wait()
-    own_copy(pl.ds(0, cols)).wait()
-    vlm_copy(pl.ds(0, cols)).wait()
-    there = act_out.at[:, pl.ds(pl.multiple_of((1 - p) * cols, cols), cols)]
-    back = pltpu.make_async_remote_copy(
-        src_ref=there, dst_ref=there, send_sem=hid_send, recv_sem=hid_recv,
-        device_id=xpart, device_id_type=MESH)
-    back.wait_send()
-    back.wait_recv()
+
+    def exchanged(cc):
+        there = act_out.at[:, out_cols(1 - p, cc)]
+        bytes_of(there, hid_send, hid_recv).wait_send()
+        bytes_of(there, hid_send, hid_recv).wait_recv()
+
+    by_width(short, copied_out)
+    by_width(short, exchanged)
+    if far:
+        @pl.when(short)
+        def _():
+            bytes_of(hid.at[:, chunk(0)], fh_send, fh_recv).wait_recv()
 
 
 def store(*refs):
@@ -328,7 +487,11 @@
                 pltpu.VMEM((vlm_rows + 2 * act_rows, features), bf16),
                 pltpu.VMEM((groups * r, cols), bf16),
                 pltpu.VMEM((vlm_rows + 2 * act_rows, cols), bf16),
-                dma, dma((4, 2)), dma((2, groups)), dma((groups, chunks)), dma, dma, dma, dma, dma((5,)), dma((3,)),
+                dma, dma((4, 2)), dma((groups + 1,)), dma((groups - 1, chunks)), dma, dma, dma, dma, dma((5,)), dma((3,)),
+                pltpu.VMEM((2 * (vr + ar), features), bf16),
+                pltpu.VMEM((groups * r, 4 * chunk_width(cols)), bf16),
+                pltpu.VMEM((2 * (vr + ar), 4 * chunk_width(cols)), bf16),
+                dma, dma, dma, dma((4,)), dma, dma,
             ],
             compiler_params=pltpu.CompilerParams(
                 collective_id=0, has_side_effects=True, vmem_limit_bytes=48 * 1024 * 1024),

time: 81.9 us -> 78.1 us (0.954)
  Pallas kernels: 81.1 us -> 77.3 us
    pallas_call x1, Pallas kernels: 79 us -> 75.2 us  [local(): pl.pallas_call(functools.partial(kernel, groups, mp_size), name='up_gelu'...]
where the time goes in v2:
time: 78.1 us; the launch traced here: 77.9 us
  Pallas kernels  77.3 us (99%)
    pallas_call x1, Pallas kernels, local(): pl.pallas_call(functools.partial(kernel, groups, mp_size), name='up_gelu'...  75.2 us
    pallas_call x1, Pallas kernels, local(): pl.pallas_call(store, name='store', out_shape=shapes, in_specs=[anywhere]...  2.03 us

profile of v2, /device:TPU:0, one launch (start us, length us, event | category | flops | bytes accessed | tf_op | source)
XLA Modules:
  0.0 77.9 jit_solution(5002080094875564451)
XLA Ops:
  0.6 75.2 %up_gelu.1 = (bf16[512,1024]{1,0:T(8,128)(2,1)S(1)}, bf16[512,2048]{1,0:T(8,128)(2,1)S(1)}, bf16[256,2048]{1,0:T(8,128)(2,1)S(1)}) custom-call(bf16[64,2048]{1,0:T(8,128)(2,1)} %vlm_hbm.1, bf16[128,2048]{1,0:T(8,128)(2,1)} %act_hbm.1, f32[1,2048]{1,0:T(1,128)} %bitcast.1, bf16[512,1024]{1,0:T(8,128)(2,1)} %proj_hbm.1), custom_call_target="tpu_custom_call" | custom-call | tf_op jit(solution)/shard_map/up_gelu/pallas_call | solution.py:477
  75.9 2.0 %store.1 = (bf16[512,1024]{1,0:T(8,128)(2,1)}, bf16[512,2048]{1,0:T(8,128)(2,1)}, bf16[256,2048]{1,0:T(8,128)(2,1)}) custom-call(bf16[512,1024]{1,0:T(8,128)(2,1)S(1)} %get-tuple-element.6.refs_0_, bf16[512,2048]{1,0:T(8,128)(2,1)S(1)} %get-tuple-element.7.refs_1_, bf16[256,2048]{1,0:T(8,128)(2,1)S(1)} %get-tuple-element.8.refs_2_), custom_call_target="tpu_custom_call" | custom-call | tf_op jit(solution)/shard_map/store/pallas_call | solution.py:500

commit v3 on v2

--- a/solution.py
+++ b/solution.py
@@ -28,7 +28,7 @@
 def kernel(groups, mp_size, vlm_hbm, act_hbm, gain_hbm, proj_hbm, vlm_out, act_out, new_out,
            vlm_ref, act_ref, gain_ref, tok, wbuf, hid, tok_send, tok_recv, w_send, w_recv, ex_send, ex_recv,
            hid_send, hid_recv, load_sem, loc_sem, far_tok, far_w, far_hid, ft_send, ft_recv, fw_send, fw_recv,
-           fh_send, fh_recv):
+           fh_send, fh_recv, ready):
     d = lax.axis_index("dp")
     m = lax.axis_index("mp")
     g, p = d // 2, d % 2
@@ -44,6 +44,7 @@
     ypart = (d, (1 - y) * 2 + c)
     has_left, has_right = g > 0, g < groups - 1
     far = groups >= 4 and n >= 8
+    late = 2
     end = (g == 0) | (g == groups - 1)
     near = ((g == 1) | (g == groups - 2)) & far
     short = end & (c == 0) & far
@@ -58,45 +59,53 @@
 
     barrier = pltpu.get_barrier_semaphore()
 
-    @pl.when(has_left)
-    def _():
-        pl.semaphore_signal(barrier, inc=1, device_id=(d - 2, m), device_id_type=MESH)
-
-    @pl.when(has_right)
-    def _():
-        pl.semaphore_signal(barrier, inc=1, device_id=(d + 2, m), device_id_type=MESH)
-
-    for other in (xpart, ypart, sibling):
-        pl.semaphore_signal(barrier, inc=1, device_id=other, device_id_type=MESH)
-
-    first_load = pltpu.make_async_copy(proj_hbm.at[:, chunk(0)], wbuf.at[block_rows(g), chunk(0)], load_sem.at[3])
-    rest_load = pltpu.make_async_copy(
-        proj_hbm.at[:, chunk(1, n - 1)], wbuf.at[block_rows(g), chunk(1, n - 1)], load_sem.at[4])
+    left, right = (d - 2, m), (d + 2, m)
+    earlier = ((has_left, left), (p == 1, xpart), (y == 1, ypart), (c == 1, sibling))
+    later = ((has_right, right), (p == 0, xpart), (y == 0, ypart), (c == 0, sibling))
+
+    def number(flags):
+        return sum(flag.astype(jnp.int32) for flag in flags)
+
+    def greet(semaphore, others):
+        for flag, other in others:
+            @pl.when(flag)
+            def _():
+                pl.semaphore_signal(semaphore, inc=1, device_id=other, device_id_type=MESH)
+
+    greet(barrier, later + ((near & (c == 1), (toward * 2 + p, y * 2)),))
+    w_load = pltpu.make_async_copy(proj_hbm, wbuf.at[block_rows(g), :], load_sem.at[3])
     loads = [pltpu.make_async_copy(src, dst, load_sem.at[i]) for i, (src, dst) in enumerate(
         ((gain_hbm, gain_ref), (vlm_hbm, vlm_ref), (act_hbm, act_ref)))]
-    first_load.start()
-    rest_load.start()
     for load in loads:
         load.start()
-
-    @pl.when(near & (c == 1))
-    def _():
-        pl.semaphore_signal(barrier, inc=1, device_id=(toward * 2 + p, y * 2), device_id_type=MESH)
-
-    pl.semaphore_wait(barrier, 3 + sum(flag.astype(jnp.int32) for flag in (has_left, has_right, short)))
-
-    def w_copy(block, cc, recv, side):
-        return pltpu.make_async_remote_copy(
-            src_ref=wbuf.at[block_rows(block), cc],
-            dst_ref=wbuf.at[block_rows(block), cc],
-            send_sem=w_send.at[jnp.where((block == g) & (side == 0), groups, block)],
+    w_load.start()
+    pl.semaphore_wait(barrier, number([flag for flag, _ in earlier] + [short]))
+    greet(ready, earlier)
+
+    brief = (near & (g == 1) & (c == 0), near & (g == groups - 2) & (c == 0))
+    last = (near & (g == 1), near & (g == groups - 2))
+
+    def w_copy(block, cc, send, recv, side, from_hbm=False):
+        there = wbuf.at[block_rows(block), cc]
+        return pltpu.make_async_remote_copy(
+            src_ref=proj_hbm.at[:, cc] if from_hbm else there,
+            dst_ref=there,
+            send_sem=w_send.at[send],
             recv_sem=recv,
-            device_id=(d - 2 if side == 0 else d + 2, m),
+            device_id=left if side == 0 else right,
             device_id_type=MESH,
         )
 
-    def w_chunk(block, k, side):
-        return w_copy(block, chunk(k), w_recv.at[lax.rem(block - g + 2 * groups + (0 if side == 0 else -2), groups), k], side)
+    def w_slot(block, side):
+        return jnp.where((block == g) & (side == 0), groups, block)
+
+    def w_last(block, side):
+        return last[side] & (block == (groups - 1 if side == 0 else 0))
+
+    def w_chunk(block, k, side, from_hbm=False):
+        return w_copy(
+            block, chunk(k), jnp.where(w_last(block, side) & (k >= n - late), groups + 1, w_slot(block, side)),
+            w_recv.at[lax.rem(block - g + 2 * groups + (0 if side == 0 else -2), groups), k], side, from_hbm)
 
     def w_arrival(block, k):
         there = wbuf.at[block_rows(block), chunk(k)]
@@ -105,24 +114,34 @@
             recv_sem=w_recv.at[lax.rem(block - g + 2 * groups - 1, groups), k],
             device_id=sibling, device_id_type=MESH)
 
-    short_left = near & (g == 1) & (c == 0)
-    short_right = near & (g == groups - 2) & (c == 0)
-
-    def send_w(block, k, side):
-        ok, brief = (has_left, short_left) if side == 0 else (has_right, short_right)
-
-        @pl.when(ok & jnp.logical_not(brief & (k == 0)))
-        def _():
-            w_chunk(block, k, side).start()
+    def send_w(block, k, side, from_hbm=False):
+        ok = has_left if side == 0 else has_right
+
+        @pl.when(ok & jnp.logical_not(brief[side] & (k == 0)))
+        def _():
+            w_chunk(block, k, side, from_hbm).start()
 
     def send_own(k):
         send_w(g, k, 0)
         send_w(g, k, 1)
 
-    first_load.wait()
-    send_own(0)
-    rest_load.wait()
-    send_own(1)
+    for k in (0, 1):
+        send_w(g, k, 0, True)
+    answers = number([flag for flag, _ in later])
+
+    @pl.when(answers > 0)
+    def _():
+        pl.semaphore_wait(ready, answers)
+
+    for k in (0, 1):
+        send_w(g, k, 1, True)
+    w_load.wait()
+    for side in (0, 1):
+        @pl.when(brief[side])
+        def _():
+            for k in (2, 3):
+                send_w(g, k, side)
+
 
     @pl.when(end)
     def _():
@@ -270,26 +289,57 @@
         wbuf.at[pl.ds(pl.multiple_of(g * r + p * half, half), half), :],
         new_out.at[:, pl.ds(pl.multiple_of(p * cols, cols), cols)], loc_sem.at[0])
 
+    def arrive_at(t, i):
+        k = t - i
+        inside = (k >= 0) & (k < n) & jnp.logical_not(short & (k == 0))
+
+        @pl.when(inside & (g - 1 - i >= 0))
+        def _():
+            w_arrival(g - 1 - i, k).wait_recv()
+            send_w(g - 1 - i, k, 1)
+
+        @pl.when(inside & (g + 1 + i < groups))
+        def _():
+            w_arrival(g + 1 + i, k).wait_recv()
+            send_w(g + 1 + i, k, 0)
+
+    def send_next(t):
+        for side in (0, 1):
+            ahead = jnp.where(brief[side] & (t < 2), 4, jnp.where(last[side] & (t >= 2), 1, 2))
+            k = jnp.where(last[side] & (t == n - 1), t, t + ahead)
+            pause = last[side] & ((t == 2) | (t == n - 2)) | brief[side] & (t >= 2) & (t < n - 3)
+
+            @pl.when((k < n) & jnp.logical_not(end) & jnp.logical_not(pause))
+            def _():
+                send_w(g, k, side)
+
+    def arrive_far(t):
+        arrive_at(t, groups - 2)
+
+    def arrive_near(t):
+        @pl.loop(0, groups - 3)
+        def _(i):
+            arrive_at(t, groups - 3 - i)
+
+        held = end & far & (t >= n - 1)
+
+        @pl.when(jnp.logical_not(held))
+        def _():
+            arrive_at(t, 0)
+
+        if t == n:
+            @pl.when(held)
+            def _():
+                arrive_at(n - 1, 0)
+
+        send_next(t)
+
     def arrive(t):
-        @pl.when((t + 2 < n) & jnp.logical_not(end))
-        def _():
-            send_own(t + 2)
-
         @pl.loop(0, groups - 1)
         def _(i):
-            k = t - i
-
-            inside = (k >= 0) & (k < n) & jnp.logical_not(short & (k == 0))
-
-            @pl.when(inside & (g - 1 - i >= 0))
-            def _():
-                w_arrival(g - 1 - i, k).wait_recv()
-                send_w(g - 1 - i, k, 1)
-
-            @pl.when(inside & (g + 1 + i < groups))
-            def _():
-                w_arrival(g + 1 + i, k).wait_recv()
-                send_w(g + 1 + i, k, 0)
+            arrive_at(t, i)
+
+        send_next(t)
 
     tile = math.gcd(256, math.gcd(vlm_rows, act_rows))
     a_tiles, v_tiles = act_rows // tile, vlm_rows // tile
@@ -339,44 +389,49 @@
     relay_first()
     if far:
         spread_far_w()
-    ex.start()
+
+    @pl.when(jnp.logical_not(near))
+    def _():
+        ex.start()
+
     kept.start()
     arrive(warm)
     arrive(warm + 1)
     relay_second()
+    arrive(warm + 2)
     if far:
         relay_far_w()
+
+    @pl.when(near)
+    def _():
+        ex.start()
+
     all_tokens()
 
-    def first_pair():
-        if far:
+    def pair_at(j, body):
+        if far and j == 0:
             @pl.when(short)
             def _():
-                for_partner(chunk(1))
-                for_self(chunk(1))
+                body(chunk(1))
 
             @pl.when(jnp.logical_not(short))
             def _():
-                for_partner(chunk(0, 2))
-                for_self(chunk(0, 2))
+                body(chunk(0, 2))
         else:
-            for_partner(chunk(0, 2))
-            for_self(chunk(0, 2))
-
-    first_pair()
-    for j in range(2, n - 2, 2):
-        for t in (warm + j - 1, warm + j):
-            if t > warm + 1:
-                arrive(t)
-        for_partner(chunk(j, 2))
-        for_self(chunk(j, 2))
-    arrive(warm + n - 3)
-    for_partner(chunk(n - 2))
-    arrive(warm + n - 2)
-    if far:
-        far_compute()
-    for_partner(chunk(n - 1))
-    for_self(chunk(n - 2, 2))
+            body(chunk(j, 2))
+
+    for j in range(0, 4, 2):
+        pair_at(j, for_partner)
+    for j in range(0, 4, 2):
+        pair_at(j, for_self)
+    for j in range(4, n):
+        arrive_far(warm + j - 1)
+        if far and j == n - 1:
+            far_compute()
+        for_partner(chunk(j))
+        arrive_near(warm + j - 1)
+        if j % 2 == 1:
+            for_self(chunk(j - 1, 2))
 
     tail_cols, all_cols = chunk(1, n - 1), chunk(0, n)
 
@@ -399,15 +454,24 @@
 
     by_width(short, copy_out)
 
+    def w_sent(block, side):
+        for skip in (0, 1):
+            for fewer in (0, late):
+                few = w_last(block, side)
+
+                @pl.when((brief[side] if skip else jnp.logical_not(brief[side])) & (few if fewer else jnp.logical_not(few)))
+                def _():
+                    w_copy(block, chunk(0, n - skip - fewer), w_slot(block, side), ex_recv, side).wait_send()
+
     @pl.loop(0, groups)
     def _(block):
         @pl.when(has_left & (block >= g))
         def _():
-            by_width(short_left, lambda cc: w_copy(block, cc, ex_recv, 0).wait_send())
+            w_sent(block, 0)
 
         @pl.when(has_right & (block <= g))
         def _():
-            by_width(short_right, lambda cc: w_copy(block, cc, ex_recv, 1).wait_send())
+            w_sent(block, 1)
 
     def bytes_of(ref, send, recv):
         return pltpu.make_async_remote_copy(
@@ -424,6 +488,10 @@
         @pl.when(near & (c == 0))
         def _():
             bytes_of(wbuf.at[:, pl.ds(0, 3 * width)], fw_send, ex_recv).wait_send()
+
+        @pl.when(near)
+        def _():
+            bytes_of(wbuf.at[pl.ds(0, r), chunk(0, late)], w_send.at[groups + 1], ex_recv).wait_send()
 
         @pl.when(end)
         def _():
@@ -487,11 +555,11 @@
                 pltpu.VMEM((vlm_rows + 2 * act_rows, features), bf16),
                 pltpu.VMEM((groups * r, cols), bf16),
                 pltpu.VMEM((vlm_rows + 2 * act_rows, cols), bf16),
-                dma, dma((4, 2)), dma((groups + 1,)), dma((groups - 1, chunks)), dma, dma, dma, dma, dma((5,)), dma((3,)),
+                dma, dma((4, 2)), dma((groups + 2,)), dma((groups - 1, chunks)), dma, dma, dma, dma, dma((4,)), dma((3,)),
                 pltpu.VMEM((2 * (vr + ar), features), bf16),
                 pltpu.VMEM((groups * r, 4 * chunk_width(cols)), bf16),
                 pltpu.VMEM((2 * (vr + ar), 4 * chunk_width(cols)), bf16),
-                dma, dma, dma, dma((4,)), dma, dma,
+                dma, dma, dma, dma((4,)), dma, dma, pltpu.SemaphoreType.REGULAR,
             ],
             compiler_params=pltpu.CompilerParams(
                 collective_id=0, has_side_effects=True, vmem_limit_bytes=48 * 1024 * 1024),

time: 78.1 us -> 77.1 us (0.987)
  Pallas kernels: 77.3 us -> 76.3 us
    pallas_call x1, Pallas kernels: 75.2 us -> 74.3 us  [local(): pl.pallas_call(functools.partial(kernel, groups, mp_size), name='up_gelu'...]
where the time goes in v3:
time: 77.1 us; the launch traced here: 76.9 us
  Pallas kernels  76.3 us (99%)
    pallas_call x1, Pallas kernels, local(): pl.pallas_call(functools.partial(kernel, groups, mp_size), name='up_gelu'...  74.3 us
    pallas_call x1, Pallas kernels, local(): pl.pallas_call(store, name='store', out_shape=shapes, in_specs=[anywhere]...  2.03 us

profile of v3, /device:TPU:0, one launch (start us, length us, event | category | flops | bytes accessed | tf_op | source)
XLA Modules:
  0.0 76.9 jit_solution(10627779316802082514)
XLA Ops:
  0.6 74.3 %up_gelu.1 = (bf16[512,1024]{1,0:T(8,128)(2,1)S(1)}, bf16[512,2048]{1,0:T(8,128)(2,1)S(1)}, bf16[256,2048]{1,0:T(8,128)(2,1)S(1)}) custom-call(bf16[64,2048]{1,0:T(8,128)(2,1)} %vlm_hbm.1, bf16[128,2048]{1,0:T(8,128)(2,1)} %act_hbm.1, f32[1,2048]{1,0:T(1,128)} %bitcast.1, bf16[512,1024]{1,0:T(8,128)(2,1)} %proj_hbm.1), custom_call_target="tpu_custom_call" | custom-call | tf_op jit(solution)/shard_map/up_gelu/pallas_call | solution.py:545
  74.9 2.0 %store.1 = (bf16[512,1024]{1,0:T(8,128)(2,1)}, bf16[512,2048]{1,0:T(8,128)(2,1)}, bf16[256,2048]{1,0:T(8,128)(2,1)}) custom-call(bf16[512,1024]{1,0:T(8,128)(2,1)S(1)} %get-tuple-element.6.refs_0_, bf16[512,2048]{1,0:T(8,128)(2,1)S(1)} %get-tuple-element.7.refs_1_, bf16[256,2048]{1,0:T(8,128)(2,1)S(1)} %get-tuple-element.8.refs_2_), custom_call_target="tpu_custom_call" | custom-call | tf_op jit(solution)/shard_map/store/pallas_call | solution.py:568

commit v4 on v3

--- a/solution.py
+++ b/solution.py
@@ -185,7 +185,7 @@
 
     def far_token_copy(part, c_from):
         rows = token_rows(p, m)[part]
-        at = pl.ds(pl.multiple_of(c_from * (vr + ar) + part * vr, math.gcd(vr, ar)), (vr, ar)[part])
+        at = pl.ds(pl.multiple_of(c_from * ar + 2 * vr if part else c_from * vr, math.gcd(vr, ar)), (vr, ar)[part])
         return pltpu.make_async_remote_copy(
             src_ref=tok.at[rows, :], dst_ref=far_tok.at[at, :], send_sem=ft_send, recv_sem=ft_recv,
             device_id=(inward * 2 + p, y * 2 + 1), device_id_type=MESH)
@@ -215,25 +215,22 @@
             far_w_copy(y * 2 + 1 - p, ypart, 1).wait_recv()
             far_w_copy(y * 2 + 1 - p, ypart, 3).start()
 
-    def far_hid_copies(same_chip):
-        for c_from in (0, 1):
-            base = c_from * (vr + ar)
-            m_from = y * 2 + c_from
-            for step_y in (0, 1):
-                y_to = y if step_y == 0 else 1 - y
-                for step_p in (0, 1):
-                    b = p if step_p == 0 else 1 - p
-                    cols_at = pl.ds(pl.multiple_of((y_to * 2 + b) * width, width), width)
-                    if (step_y == 0 and step_p == 0) == same_chip:
-                        yield pltpu.make_async_remote_copy(
-                            src_ref=far_hid.at[pl.ds(base, vr), cols_at],
-                            dst_ref=vlm_out.at[pl.ds(pl.multiple_of((p * mp_size + m_from) * vr, vr), vr), chunk(0)],
-                            send_sem=fh_send, recv_sem=fh_recv, device_id=(toward * 2 + b, y_to * 2), device_id_type=MESH)
-                    if (step_y == 0) == same_chip:
-                        yield pltpu.make_async_remote_copy(
-                            src_ref=far_hid.at[pl.ds(base + vr, ar), cols_at],
-                            dst_ref=act_out.at[pl.ds(pl.multiple_of(m_from * ar, ar), ar), out_cols(b, chunk(0))],
-                            send_sem=fh_send, recv_sem=fh_recv, device_id=(toward * 2 + p, y_to * 2), device_id_type=MESH)
+    def far_hid_copies(phase):
+        for step_y in (0, 1):
+            y_to = y if step_y == 0 else 1 - y
+            for step_p in (0, 1):
+                b = p if step_p == 0 else 1 - p
+                cols_at = pl.ds(pl.multiple_of((y_to * 2 + b) * width, width), width)
+                if 1 + step_y == phase:
+                    yield pltpu.make_async_remote_copy(
+                        src_ref=far_hid.at[pl.ds(2 * vr, 2 * ar), cols_at],
+                        dst_ref=act_out.at[pl.ds(pl.multiple_of(y * 2 * ar, 2 * ar), 2 * ar), out_cols(b, chunk(0))],
+                        send_sem=fh_send, recv_sem=fh_recv, device_id=(toward * 2 + p, y_to * 2), device_id_type=MESH)
+                if (0 if step_p else 1 + step_y) == phase:
+                    yield pltpu.make_async_remote_copy(
+                        src_ref=far_hid.at[pl.ds(0, 2 * vr), cols_at],
+                        dst_ref=vlm_out.at[pl.ds(pl.multiple_of((p * mp_size + y * 2) * vr, 2 * vr), 2 * vr), chunk(0)],
+                        send_sem=fh_send, recv_sem=fh_recv, device_id=(toward * 2 + b, y_to * 2), device_id_type=MESH)
 
     def far_compute():
         @pl.when(near & (c == 1))
@@ -255,7 +252,7 @@
                     pre = jnp.dot(far_tok[rows, :], far_w[:, at], preferred_element_type=jnp.float32)
                     far_hid[rows, at] = gelu(pre)
 
-            for copy in far_hid_copies(True):
+            for copy in far_hid_copies(0):
                 copy.start()
 
     def relay_first():
@@ -426,8 +423,14 @@
         pair_at(j, for_self)
     for j in range(4, n):
         arrive_far(warm + j - 1)
+        if far and j == n - 2:
+            far_compute()
         if far and j == n - 1:
-            far_compute()
+            @pl.when(near & (c == 1))
+            def _():
+                for copy in far_hid_copies(1):
+                    copy.start()
+
         for_partner(chunk(j))
         arrive_near(warm + j - 1)
         if j % 2 == 1:
@@ -463,13 +466,24 @@
                 def _():
                     w_copy(block, chunk(0, n - skip - fewer), w_slot(block, side), ex_recv, side).wait_send()
 
+    if far:
+        @pl.when(near & (c == 1))
+        def _():
+            for side in (0, 1):
+                @pl.when(last[side])
+                def _():
+                    w_sent(groups - 1 if side == 0 else 0, side)
+
+            for copy in far_hid_copies(2):
+                copy.start()
+
     @pl.loop(0, groups)
     def _(block):
-        @pl.when(has_left & (block >= g))
+        @pl.when(has_left & (block >= g) & jnp.logical_not(w_last(block, 0) & (c == 1)))
         def _():
             w_sent(block, 0)
 
-        @pl.when(has_right & (block <= g))
+        @pl.when(has_right & (block <= g) & jnp.logical_not(w_last(block, 1) & (c == 1)))
         def _():
             w_sent(block, 1)
 
@@ -480,8 +494,6 @@
     if far:
         @pl.when(near & (c == 1))
         def _():
-            for copy in far_hid_copies(False):
-                copy.start()
             bytes_of(far_w.at[:, pl.ds(0, width)], fw_send, ex_recv).wait_send()
             bytes_of(hid.at[pl.ds(0, 8 * (vr + ar)), chunk(0)], fh_send, ex_recv).wait_send()
 

time: 77.1 us -> 76.4 us (level)
  no operation moved by 1% of the time
where the time goes in v4:
time: 76.4 us; the launch traced here: 76.3 us
  Pallas kernels  75.6 us (99%)
    pallas_call x1, Pallas kernels, local(): pl.pallas_call(functools.partial(kernel, groups, mp_size), name='up_gelu'...  73.6 us
    pallas_call x1, Pallas kernels, local(): pl.pallas_call(store, name='store', out_shape=shapes, in_specs=[anywhere]...  2.03 us

profile of v4, /device:TPU:0, one launch (start us, length us, event | category | flops | bytes accessed | tf_op | source)
XLA Modules:
  0.0 76.3 jit_solution(16717781062864193792)
XLA Ops:
  0.6 73.6 %up_gelu.1 = (bf16[512,1024]{1,0:T(8,128)(2,1)S(1)}, bf16[512,2048]{1,0:T(8,128)(2,1)S(1)}, bf16[256,2048]{1,0:T(8,128)(2,1)S(1)}) custom-call(bf16[64,2048]{1,0:T(8,128)(2,1)} %vlm_hbm.1, bf16[128,2048]{1,0:T(8,128)(2,1)} %act_hbm.1, f32[1,2048]{1,0:T(1,128)} %bitcast.1, bf16[512,1024]{1,0:T(8,128)(2,1)} %proj_hbm.1), custom_call_target="tpu_custom_call" | custom-call | tf_op jit(solution)/shard_map/up_gelu/pallas_call | solution.py:557
  74.2 2.0 %store.1 = (bf16[512,1024]{1,0:T(8,128)(2,1)}, bf16[512,2048]{1,0:T(8,128)(2,1)}, bf16[256,2048]{1,0:T(8,128)(2,1)}) custom-call(bf16[512,1024]{1,0:T(8,128)(2,1)S(1)} %get-tuple-element.6.refs_0_, bf16[512,2048]{1,0:T(8,128)(2,1)S(1)} %get-tuple-element.7.refs_1_, bf16[256,2048]{1,0:T(8,128)(2,1)S(1)} %get-tuple-element.8.refs_2_), custom_call_target="tpu_custom_call" | custom-call | tf_op jit(solution)/shard_map/store/pallas_call | solution.py:580

commit v5 on v4

--- a/solution.py
+++ b/solution.py
@@ -60,8 +60,9 @@
     barrier = pltpu.get_barrier_semaphore()
 
     left, right = (d - 2, m), (d + 2, m)
-    earlier = ((has_left, left), (p == 1, xpart), (y == 1, ypart), (c == 1, sibling))
-    later = ((has_right, right), (p == 0, xpart), (y == 0, ypart), (c == 0, sibling))
+    leads = ((g == 0) & (c == 0)) | ((g > 0) & (c == 1))
+    earlier = ((has_left, left), (p == 1, xpart), (y == 1, ypart), (jnp.logical_not(leads), sibling))
+    later = ((has_right, right), (p == 0, xpart), (y == 0, ypart), (leads, sibling))
 
     def number(flags):
         return sum(flag.astype(jnp.int32) for flag in flags)

time: 76.4 us -> 76 us (level)
  no operation moved by 1% of the time
where the time goes in v5:
time: 76 us; the launch traced here: 75.8 us
  Pallas kernels  75.2 us (99%)
    pallas_call x1, Pallas kernels, local(): pl.pallas_call(functools.partial(kernel, groups, mp_size), name='up_gelu'...  73.2 us
    pallas_call x1, Pallas kernels, local(): pl.pallas_call(store, name='store', out_shape=shapes, in_specs=[anywhere]...  2.03 us

profile of v5, /device:TPU:0, one launch (start us, length us, event | category | flops | bytes accessed | tf_op | source)
XLA Modules:
  0.0 75.8 jit_solution(4043071170242978258)
XLA Ops:
  0.6 73.2 %up_gelu.1 = (bf16[512,1024]{1,0:T(8,128)(2,1)S(1)}, bf16[512,2048]{1,0:T(8,128)(2,1)S(1)}, bf16[256,2048]{1,0:T(8,128)(2,1)S(1)}) custom-call(bf16[64,2048]{1,0:T(8,128)(2,1)} %vlm_hbm.1, bf16[128,2048]{1,0:T(8,128)(2,1)} %act_hbm.1, f32[1,2048]{1,0:T(1,128)} %bitcast.1, bf16[512,1024]{1,0:T(8,128)(2,1)} %proj_hbm.1), custom_call_target="tpu_custom_call" | custom-call | tf_op jit(solution)/shard_map/up_gelu/pallas_call | solution.py:558
  73.8 2.0 %store.1 = (bf16[512,1024]{1,0:T(8,128)(2,1)}, bf16[512,2048]{1,0:T(8,128)(2,1)}, bf16[256,2048]{1,0:T(8,128)(2,1)}) custom-call(bf16[512,1024]{1,0:T(8,128)(2,1)S(1)} %get-tuple-element.6.refs_0_, bf16[512,2048]{1,0:T(8,128)(2,1)S(1)} %get-tuple-element.7.refs_1_, bf16[256,2048]{1,0:T(8,128)(2,1)S(1)} %get-tuple-element.8.refs_2_), custom_call_target="tpu_custom_call" | custom-call | tf_op jit(solution)/shard_map/store/pallas_call | solution.py:581
